TPU v7x, 32 devices: a whole 2x2x4 slice. The times are simulated.
32 devices in a mesh: row: 8 (over y, x, core), shift: 4 (over z).
Axes of the slice: x: 2, y: 2, z: 4, core: 2. Of those that a mesh axis runs over, the one named last changes fastest.
Arguments:
- snapshots: bfloat16 [4096, 2, 128], P('row'), may hold values from -6 to 6
- tail_sensors: bfloat16 [128, 2, 128], replicated, may hold values from -6 to 6
- shift_offsets: int32 [12], P('shift'), may hold values from 0 to 128
- start_basis: float32 [64, 4096], P(None, 'row'), may hold values from -0.09375 to 0.09375
Outputs:
- covariance: float32 [4096, 4096], P('row', 'shift')
- signal_basis: float32 [64, 4096], P(None, 'row')
Inputs may be any that keep to these rules, and one draw needn't show every extreme that they name: `shift_offsets`: each shift's first sensor.
All inputs are finite; a program needn't handle non-finite values.
Results may differ from a plain program's by a relative error of at most 0.0031.
Values may be sent and summed in bfloat16 or wider, within the bound.
A program may use at most 64 MiB of HBM per device.

v0:
```python
import jax
import jax.numpy as jnp
from jax import lax
from jax.sharding import PartitionSpec as P

M = 4096
SNAPS = 128
ITERS = 2
half_root = 0.7071067811865476


def make_some(extended, offset, start, count):
    window = lax.dynamic_slice_in_dim(extended, offset + start, count, 0).astype(jnp.float32)
    mirror = lax.dynamic_slice_in_dim(extended, offset + M - start - count, count, 0).astype(
        jnp.float32
    )[::-1]
    summed_pair = window + mirror
    difference = window - mirror
    upper_rows = jnp.concatenate([summed_pair[:, 0], summed_pair[:, 1]], axis=1)
    bottom = jnp.concatenate([difference[:, 1], -difference[:, 0]], axis=1)
    positions = start + jnp.arange(count, dtype=jnp.int32)
    chosen = jnp.where((positions < M // 2)[:, None], upper_rows, bottom)
    return (chosen * half_root).astype(jnp.bfloat16)


def factor(gram_matrix):
    lower_factor = jnp.linalg.cholesky(gram_matrix)
    identity = jnp.eye(gram_matrix.shape[0], dtype=jnp.float32)
    return jax.scipy.linalg.solve_triangular(lower_factor, identity, lower=True)


def per_device(snapshots, tail_sensors, shift_offsets, start_basis):
    block_rows = snapshots.shape[0]
    row_index = lax.axis_index("row")
    shift_index = lax.axis_index("shift")
    col_count = M // lax.axis_size("shift")
    normalizer = 1.0 / (SNAPS * shift_offsets.shape[0] * lax.axis_size("shift"))
    gathered = lax.all_gather(snapshots, "row", axis=0, tiled=True)
    extended = jnp.concatenate([gathered, tail_sensors], 0)
    every_offset = lax.all_gather(shift_offsets, "shift", axis=0, tiled=True)
    row_start = row_index * block_rows
    col_start = shift_index * col_count

    def add_block(which, running):
        offset = every_offset[which]
        own_rows = make_some(extended, offset, row_start, block_rows)
        col_rows = make_some(extended, offset, col_start, col_count)
        return running + lax.dot_general(
            own_rows, col_rows, (((1,), (1,)), ((), ())), preferred_element_type=jnp.float32
        )

    summed_block = lax.fori_loop(
        0, every_offset.shape[0], add_block, jnp.zeros((block_rows, col_count), jnp.float32)
    )
    cov_out = summed_block * normalizer
    basis_rows = lax.all_gather(start_basis, "row", axis=1, tiled=True)
    own_basis = start_basis
    for sweep in range(ITERS):
        basis_cols = lax.dynamic_slice_in_dim(basis_rows, shift_index * col_count, col_count, 1)
        column_terms = lax.dot_general(
            basis_cols, cov_out, (((1,), (1,)), ((), ())), precision=lax.Precision.HIGHEST
        )
        mapped = lax.psum(column_terms, "shift")
        local_gram = jnp.dot(mapped, mapped.T, precision=lax.Precision.HIGHEST)
        gram_matrix = lax.psum(local_gram, "row")
        own_basis = jnp.dot(factor(gram_matrix), mapped, precision=lax.Precision.HIGHEST)
        if sweep + 1 < ITERS:
            basis_rows = lax.all_gather(own_basis, "row", axis=1, tiled=True)
    return (cov_out, own_basis)


def solution(mesh):
    in_specs = (P("row", None, None), P(), P("shift"), P(None, "row"))
    out_specs = (P("row", "shift"), P(None, "row"))
    return jax.shard_map(
        per_device, mesh=mesh, in_specs=in_specs, out_specs=out_specs, check_vma=False
    )
```

profile of v0, /device:TPU:0, one launch (start us, length us, event | category | flops | bytes accessed | tf_op | source)
XLA Modules:
  0.0 375.3 jit_solution(9196168970584460465)
XLA Ops:
  8.7 1.3 dynamic-slice
  11.5 9.9 %all-reduce = s32[12]{0:T(128)S(1)} all-reduce(s32[12]{0:T(128)S(1)} %dynamic-update-slice.2), channel_id=1, replica_groups=mesh['row'=8,'shift'=4] {'shift'}, use_global_device_ids=true, to_apply=%add | all-reduce | flops 12 | bytes 96
  21.4 19.0 %all-gather.4.cloned.1.call-done = bf16[4096,2,128]{2,1,0:T(2,128)(2,1)} async-done(((bf16[512,2,128]{2,1,0:T(2,128)(2,1)}), bf16[4096,2,128]{2,1,0:T(2,128)(2,1)}) %all-gather.4.cloned.1.call-update) | async-done | bytes 2097168 | tf_op jit(solution)/shard_map/all_gather | solution.py:38
  40.4 6.4 %pad_maximum_fusion = bf16[4224,2,128]{2,1,0:T(2,128)(2,1)S(1)} fusion(bf16[128,2,128]{2,1,0:T(2,128)(2,1)} %param.10, bf16[4096,2,128]{2,1,0:T(2,128)(2,1)} %all-gather.4.cloned.1.call-done), kind=kLoop, calls=%fused_computation.31 | loop fusion | flops 1081344 | bytes 4325376 | tf_op jit(solution)/shard_map/concatenate | solution.py:39
  46.8 1.6 copy.30
  48.4 143.1 %while.18 = (s32[]{:T(128)}, f32[512,1024]{1,0:T(8,128)}, s32[]{:T(128)}, s32[12]{0:T(128)S(1)}, bf16[4224,2,128]{2,0,1:T(8,128)(2,1)}, /*index=5*/s32[]{:T(128)...) while((s32[]{:T(128)}, f32[512,1024]{1,0:T(8,128)}, ...), condition=%wide.region_1.2_spmd.clone, body=%wide.region_0.1_spmd.clone.sunk | while | flops 273222688 | bytes 47713820 | solution.py:52
  59.1 1.3 copy-done.1
  71.0 1.3 copy-done.1
  82.9 1.3 copy-done.1
  94.9 1.3 copy-done.1
  106.8 1.3 copy-done.1
  118.7 1.3 copy-done.1
  130.6 1.3 copy-done.1
  142.6 1.3 copy-done.1
  154.5 1.3 copy-done.1
  166.4 1.3 copy-done.1
  178.3 1.3 copy-done.1
  190.3 1.3 copy-done.1
  191.6 1.8 broadcast_multiply_fusion
  193.4 4.0 %fusion.16 = f32[64,512]{1,0:T(8,128)} fusion(f32[512,1024]{1,0:T(8,128)S(1)} %broadcast_multiply_fusion, f32[64,4096]{1,0:T(8,128)} %all-gather.6.cloned.1.call-done, s32[]{:T(128)S(6)} %select_n.96), kind=kOutput, calls=%fused_computation.35 | convolution fusion | flops 402653184 | bytes 2490372 | tf_op jit(solution)/shard_map/dot_general | solution.py:60
  197.5 34.7 %all-reduce.4.cloned.1.call-done = f32[64,512]{1,0:T(8,128)} async-done(((f32[64,512]{1,0:T(8,128)}), f32[64,512]{1,0:T(8,128)}) %all-reduce.4.cloned.1.call-update) | async-done | bytes 131088 | tf_op jit(solution)/shard_map/psum | solution.py:63
  233.4 22.4 %psum.29 = f32[64,64]{0,1:T(8,128)S(1)} all-reduce(f32[64,64]{0,1:T(8,128)S(1)} %fusion.32), channel_id=1, replica_groups=mesh['row'=8,'shift'=4] {'row'}, use_global_device_ids=true, to_apply=%region_3.4 | all-reduce | flops 4096 | bytes 32768 | tf_op jit(solution)/shard_map/psum | solution.py:65
  255.9 5.8 %cholesky.44 = f32[64,64]{1,0:T(8,128)S(1)} custom-call(f32[64,64]{1,0:T(8,128)S(1)} %fusion.27), custom_call_target="Cholesky" | custom-call | tf_op jit(solution)/shard_map/jit(cholesky)/cholesky | solution.py:27
  263.1 4.9 %custom-call.7 = f32[1,64,64]{1,2,0:T(8,128)S(1)} custom-call(f32[1,64,64]{2,1,0:T(8,128)S(1)} %fusion.22), custom_call_target="InvertDiagBlocksLowerTriangular" | custom-call | tf_op jit(solution)/shard_map/jit(_solve_triangular)/triangular_solve | solution.py:29
  268.2 1.8 fusion.33
  270.1 22.3 %all-gather.8.cloned.1.call-done = f32[64,4096]{1,0:T(8,128)} async-done(((f32[64,512]{1,0:T(8,128)}), f32[64,4096]{1,0:T(8,128)}) %all-gather.8.cloned.1.call-update) | async-done | bytes 1048592 | tf_op jit(solution)/shard_map/all_gather | solution.py:68
  292.4 3.7 fusion.14
  296.2 34.8 %all-reduce.6.cloned.1.call-done = f32[64,512]{1,0:T(8,128)} async-done(((f32[64,512]{1,0:T(8,128)}), f32[64,512]{1,0:T(8,128)}) %all-reduce.6.cloned.1.call-update) | async-done | bytes 131088 | tf_op jit(solution)/shard_map/psum | solution.py:63
  332.2 22.4 %psum.31 = f32[64,64]{0,1:T(8,128)S(1)} all-reduce(f32[64,64]{0,1:T(8,128)S(1)} %fusion.34), channel_id=1, replica_groups=mesh['row'=8,'shift'=4] {'row'}, use_global_device_ids=true, to_apply=%region_7.10 | all-reduce | flops 4096 | bytes 32768 | tf_op jit(solution)/shard_map/psum | solution.py:65
  354.6 5.8 %cholesky.55 = f32[64,64]{1,0:T(8,128)S(1)} custom-call(f32[64,64]{1,0:T(8,128)S(1)} %fusion.25), custom_call_target="Cholesky" | custom-call | tf_op jit(solution)/shard_map/jit(cholesky)/cholesky | solution.py:27
  361.8 4.9 %custom-call.8 = f32[1,64,64]{1,2,0:T(8,128)S(1)} custom-call(f32[1,64,64]{2,1,0:T(8,128)S(1)} %fusion.23), custom_call_target="InvertDiagBlocksLowerTriangular" | custom-call | tf_op jit(solution)/shard_map/jit(_solve_triangular)/triangular_solve | solution.py:29
  367.0 1.8 fusion.35
  (282 shorter events, 109.5 us)
Async XLA Ops:
  7.2 33.2 %all-gather.4.cloned.1.call-start = ((), (), s32[]{:S(2)}) async-start(), calls=%async_computation | async-start | bytes 2359296 | tf_op jit(solution)/shard_map/all_gather | solution.py:38
  7.9 185.5 %all-gather.6.cloned.1.call-start = ((), (), s32[]{:S(2)}) async-start(), calls=%async_computation.1 | async-start | bytes 1179648 | tf_op jit(solution)/shard_map/all_gather | solution.py:56
  8.6 223.5 %all-reduce.4.cloned.1.call-start = ((), (), s32[]{:S(2)}) async-start(), calls=%async_computation.2 | async-start | bytes 262144 | tf_op jit(solution)/shard_map/psum | solution.py:63
  55.7 2.1 copy-start
  56.5 1.4 copy-start.3
  56.5 1.6 copy-start.4
  67.6 2.1 copy-start
  68.4 1.4 copy-start.3
  68.4 1.6 copy-start.4
  79.5 2.1 copy-start
  80.4 1.6 copy-start.4
  91.5 2.1 copy-start
  92.3 1.6 copy-start.4
  103.4 2.1 copy-start
  104.2 1.6 copy-start.4
  115.3 2.1 copy-start
  116.1 1.6 copy-start.4
  127.2 2.1 copy-start
  128.1 1.6 copy-start.4
  139.2 2.1 copy-start
  140.0 1.6 copy-start.4
  151.1 2.1 copy-start
  151.9 1.6 copy-start.4
  163.0 2.1 copy-start
  163.8 1.6 copy-start.4
  174.9 2.1 copy-start
  175.8 1.6 copy-start.4
  186.9 2.1 copy-start
  187.7 1.6 copy-start.4
  193.4 102.8 %copy-start.5 = (f32[512,1024]{1,0:T(8,128)}, f32[512,1024]{1,0:T(8,128)S(1)}, u32[]{:S(2)}) copy-start(f32[512,1024]{1,0:T(8,128)S(1)} %broadcast_multiply_fusion) | copy-start | bytes 6291460
  197.4 95.0 %all-gather.8.cloned.1.call-start = ((), (), s32[]{:S(2)}) async-start(), calls=%async_computation.3 | async-start | bytes 1179648 | tf_op jit(solution)/shard_map/all_gather | solution.py:68
  270.1 60.9 %all-reduce.6.cloned.1.call-start = ((), (), s32[]{:S(2)}) async-start(), calls=%async_computation.4 | async-start | bytes 262144 | tf_op jit(solution)/shard_map/psum | solution.py:63
  (34 other events, 45.8 us)
Sparse Core Ops, SparseCore 0:
  9.9 30.4 all-gather.3
  42.3 23.3 all-gather.5
  197.5 34.6 all-reduce.3
  270.2 22.1 all-gather.7
  296.3 34.6 all-reduce.5
where the time goes:
time: 378 us; the launch traced here: 375 us
  waiting for transfers between devices  112 us (30%)
  other arithmetic  102 us (27%)
  blocking collectives  54.6 us (14%)
  local copies, waits for them, and re-layouts  39.1 us (10%)
  loops' own time  26.2 us (7%)
  matrix products  26 us (7%)
  between operations  14.5 us (4%)
    psum x2, waiting for transfers between devices, per_device(): mapped = lax.psum(column_terms, 'shift')  69.5 us
    psum x2, blocking collectives, per_device(): gram_matrix = lax.psum(local_gram, 'row')  44.7 us
    sub x24, other arithmetic, make_some(): difference = window - mirror  28.7 us
    another operation x1, loops' own time, per_device(): lax.fori_loop(0, every_offset.shape[0], add_block, jnp.zeros((block_rows,...  26.2 us
    convert_element_type x24, other arithmetic, make_some(): lax.dynamic_slice_in_dim(extended, offset + M - start - count, count, 0)  26 us
    all_gather x1, waiting for transfers between devices, per_device(): basis_rows = lax.all_gather(own_basis, 'row', axis=1, tiled=True)  22.3 us
    while x120, local copies, waits for them, and re-layouts  19.4 us
    all_gather x1, waiting for transfers between devices, per_device(): gathered = lax.all_gather(snapshots, 'row', axis=0, tiled=True)  19 us
  transfers between devices with their start and end apart: 5, of which 4 were waited for; matrix products, arithmetic and copies ran while one was open for 29% of the time, Pallas kernels for 0%

commit v1 on v0

--- a/solution.py
+++ b/solution.py
@@ -60,7 +60,7 @@
         column_terms = lax.dot_general(
             basis_cols, cov_out, (((1,), (1,)), ((), ())), precision=lax.Precision.HIGHEST
         )
-        mapped = lax.psum(column_terms, "shift")
+        mapped = jnp.sum(lax.all_gather(column_terms, "shift"), axis=0)
         local_gram = jnp.dot(mapped, mapped.T, precision=lax.Precision.HIGHEST)
         gram_matrix = lax.psum(local_gram, "row")
         own_basis = jnp.dot(factor(gram_matrix), mapped, precision=lax.Precision.HIGHEST)

time: 378 us -> 337 us (0.89)
  waiting for transfers between devices: 112 us -> 44.3 us
  blocking collectives: 54.6 us -> 86.7 us
  matrix products: 26 us -> 20.9 us
    psum x2 -> x0, waiting for transfers between devices: 69.5 us -> none  [per_device(): mapped = lax.psum(column_terms, 'shift')]
    all_gather x0 -> x2, blocking collectives: none -> 32 us  [per_device(): mapped = jnp.sum(lax.all_gather(column_terms, 'shift'), axis=0)]
  transfers between devices with their start and end apart: 5 -> 3, of which waited for: 4 -> 2; matrix products, arithmetic and copies ran while one was open for 29% -> 33% of each run, Pallas kernels for 0% -> 0%
where the time goes in v1:
time: 337 us; the launch traced here: 334 us
  other arithmetic  102 us (30%)
  blocking collectives  86.7 us (26%)
  waiting for transfers between devices  44.3 us (13%)
  local copies, waits for them, and re-layouts  39.1 us (12%)
  loops' own time  26.2 us (8%)
  matrix products  20.9 us (6%)
  between operations  14.5 us (4%)
    psum x2, blocking collectives, per_device(): gram_matrix = lax.psum(local_gram, 'row')  44.7 us
    all_gather x2, blocking collectives, per_device(): mapped = jnp.sum(lax.all_gather(column_terms, 'shift'), axis=0)  32 us
    sub x24, other arithmetic, make_some(): difference = window - mirror  28.7 us
    another operation x1, loops' own time, per_device(): lax.fori_loop(0, every_offset.shape[0], add_block, jnp.zeros((block_rows,...  26.2 us
    convert_element_type x24, other arithmetic, make_some(): lax.dynamic_slice_in_dim(extended, offset + M - start - count, count, 0)  26 us
    all_gather x1, waiting for transfers between devices, per_device(): basis_rows = lax.all_gather(own_basis, 'row', axis=1, tiled=True)  23.9 us
    while x120, local copies, waits for them, and re-layouts  19.4 us
    all_gather x1, waiting for transfers between devices, per_device(): gathered = lax.all_gather(snapshots, 'row', axis=0, tiled=True)  19 us
  transfers between devices with their start and end apart: 3, of which 2 were waited for; matrix products, arithmetic and copies ran while one was open for 33% of the time, Pallas kernels for 0%

profile of v1, /device:TPU:0, one launch (start us, length us, event | category | flops | bytes accessed | tf_op | source)
XLA Modules:
  0.0 334.3 jit_solution(10712000800947193462)
XLA Ops:
  8.7 1.3 dynamic-slice
  11.5 9.9 %all-reduce = s32[12]{0:T(128)S(1)} all-reduce(s32[12]{0:T(128)S(1)} %dynamic-update-slice.2), channel_id=1, replica_groups=mesh['row'=8,'shift'=4] {'shift'}, use_global_device_ids=true, to_apply=%add | all-reduce | flops 12 | bytes 96
  21.4 19.0 %all-gather.6.cloned.1.call-done = bf16[4096,2,128]{2,1,0:T(2,128)(2,1)} async-done(((bf16[512,2,128]{2,1,0:T(2,128)(2,1)}), bf16[4096,2,128]{2,1,0:T(2,128)(2,1)}) %all-gather.6.cloned.1.call-update) | async-done | bytes 2097168 | tf_op jit(solution)/shard_map/all_gather | solution.py:38
  40.4 6.4 %pad_maximum_fusion = bf16[4224,2,128]{2,1,0:T(2,128)(2,1)S(1)} fusion(bf16[128,2,128]{2,1,0:T(2,128)(2,1)} %param.10, bf16[4096,2,128]{2,1,0:T(2,128)(2,1)} %all-gather.6.cloned.1.call-done), kind=kLoop, calls=%fused_computation.31 | loop fusion | flops 1081344 | bytes 4325376 | tf_op jit(solution)/shard_map/concatenate | solution.py:39
  46.8 1.6 copy.30
  48.4 143.1 %while.18 = (s32[]{:T(128)}, f32[512,1024]{1,0:T(8,128)}, s32[]{:T(128)}, s32[12]{0:T(128)S(1)}, bf16[4224,2,128]{2,0,1:T(8,128)(2,1)}, /*index=5*/s32[]{:T(128)...) while((s32[]{:T(128)}, f32[512,1024]{1,0:T(8,128)}, ...), condition=%wide.region_1.2_spmd.clone, body=%wide.region_0.1_spmd.clone.sunk | while | flops 273222688 | bytes 47713820 | solution.py:52
  52.0 1.2 convert_subtract_fusion.4
  59.1 1.3 copy-done.1
  63.9 1.2 convert_subtract_fusion.4
  71.0 1.3 copy-done.1
  82.9 1.3 copy-done.1
  94.9 1.3 copy-done.1
  106.8 1.3 copy-done.1
  118.7 1.3 copy-done.1
  130.6 1.3 copy-done.1
  142.6 1.3 copy-done.1
  154.5 1.3 copy-done.1
  166.4 1.3 copy-done.1
  178.3 1.3 copy-done.1
  190.3 1.3 copy-done.1
  191.6 1.8 broadcast_multiply_fusion
  193.4 3.3 fusion.16
  196.7 16.0 %all-gather = f32[256,512]{1,0:T(8,128)S(1)} all-gather(f32[64,512]{1,0:T(8,128)S(1)} %fusion.16), channel_id=2, replica_groups=mesh['row'=8,'shift'=4] {'shift'}, dimensions={0}, use_global_device_ids=true | all-gather | bytes 655360 | tf_op jit(solution)/shard_map/all_gather | solution.py:63
  213.1 22.4 %psum.14 = f32[64,64]{0,1:T(8,128)S(1)} all-reduce(f32[64,64]{0,1:T(8,128)S(1)} %fusion.32), channel_id=1, replica_groups=mesh['row'=8,'shift'=4] {'row'}, use_global_device_ids=true, to_apply=%region_3.4 | all-reduce | flops 4096 | bytes 32768 | tf_op jit(solution)/shard_map/psum | solution.py:65
  235.5 5.8 %cholesky.44 = f32[64,64]{1,0:T(8,128)S(1)} custom-call(f32[64,64]{1,0:T(8,128)S(1)} %fusion.27), custom_call_target="Cholesky" | custom-call | tf_op jit(solution)/shard_map/jit(cholesky)/cholesky | solution.py:27
  242.7 4.9 %custom-call.7 = f32[1,64,64]{1,2,0:T(8,128)S(1)} custom-call(f32[1,64,64]{2,1,0:T(8,128)S(1)} %fusion.22), custom_call_target="InvertDiagBlocksLowerTriangular" | custom-call | tf_op jit(solution)/shard_map/jit(_solve_triangular)/triangular_solve | solution.py:29
  248.8 23.9 %all-gather.10.cloned.1.call-done = f32[64,4096]{1,0:T(8,128)} async-done(((f32[64,512]{1,0:T(8,128)}), f32[64,4096]{1,0:T(8,128)}) %all-gather.10.cloned.1.call-update) | async-done | bytes 1048592 | tf_op jit(solution)/shard_map/all_gather | solution.py:68
  272.7 3.1 fusion.14
  275.8 16.0 %all-gather.1 = f32[256,512]{1,0:T(8,128)S(1)} all-gather(f32[64,512]{1,0:T(8,128)S(1)} %fusion.14), channel_id=3, replica_groups=mesh['row'=8,'shift'=4] {'shift'}, dimensions={0}, use_global_device_ids=true | all-gather | bytes 655360 | tf_op jit(solution)/shard_map/all_gather | solution.py:63
  292.1 22.4 %psum.15 = f32[64,64]{0,1:T(8,128)S(1)} all-reduce(f32[64,64]{0,1:T(8,128)S(1)} %fusion.34), channel_id=1, replica_groups=mesh['row'=8,'shift'=4] {'row'}, use_global_device_ids=true, to_apply=%region_7.10 | all-reduce | flops 4096 | bytes 32768 | tf_op jit(solution)/shard_map/psum | solution.py:65
  314.5 5.8 %cholesky.55 = f32[64,64]{1,0:T(8,128)S(1)} custom-call(f32[64,64]{1,0:T(8,128)S(1)} %fusion.25), custom_call_target="Cholesky" | custom-call | tf_op jit(solution)/shard_map/jit(cholesky)/cholesky | solution.py:27
  321.7 4.9 %custom-call.8 = f32[1,64,64]{1,2,0:T(8,128)S(1)} custom-call(f32[1,64,64]{2,1,0:T(8,128)S(1)} %fusion.23), custom_call_target="InvertDiagBlocksLowerTriangular" | custom-call | tf_op jit(solution)/shard_map/jit(_solve_triangular)/triangular_solve | solution.py:29
  (280 shorter events, 106.9 us)
Async XLA Ops:
  7.2 33.2 %all-gather.6.cloned.1.call-start = ((), (), s32[]{:S(2)}) async-start(), calls=%async_computation | async-start | bytes 2359296 | tf_op jit(solution)/shard_map/all_gather | solution.py:38
  7.9 185.5 %all-gather.8.cloned.1.call-start = ((), (), s32[]{:S(2)}) async-start(), calls=%async_computation.1 | async-start | bytes 1179648 | tf_op jit(solution)/shard_map/all_gather | solution.py:56
  8.6 264.0 %all-gather.10.cloned.1.call-start = ((), (), s32[]{:S(2)}) async-start(), calls=%async_computation.2 | async-start | bytes 1179648 | tf_op jit(solution)/shard_map/all_gather | solution.py:68
  55.7 2.1 copy-start
  56.5 1.4 copy-start.3
  56.5 1.6 copy-start.4
  67.6 2.1 copy-start
  68.4 1.4 copy-start.3
  68.4 1.6 copy-start.4
  79.5 2.1 copy-start
  80.4 1.4 copy-start.3
  80.4 1.6 copy-start.4
  91.5 2.1 copy-start
  92.3 1.4 copy-start.3
  92.3 1.6 copy-start.4
  103.4 2.1 copy-start
  104.2 1.6 copy-start.4
  115.3 2.1 copy-start
  116.1 1.6 copy-start.4
  127.2 2.1 copy-start
  128.1 1.6 copy-start.4
  139.2 2.1 copy-start
  140.0 1.6 copy-start.4
  151.1 2.1 copy-start
  151.9 1.6 copy-start.4
  163.0 2.1 copy-start
  163.8 1.6 copy-start.4
  174.9 2.1 copy-start
  175.8 1.6 copy-start.4
  186.9 2.1 copy-start
  187.7 1.6 copy-start.4
  193.4 79.3 %copy-start.5 = (f32[512,1024]{1,0:T(8,128)}, f32[512,1024]{1,0:T(8,128)S(1)}, u32[]{:S(2)}) copy-start(f32[512,1024]{1,0:T(8,128)S(1)} %broadcast_multiply_fusion) | copy-start | bytes 6291460
  (32 other events, 42.9 us)
Sparse Core Ops, SparseCore 0:
  9.9 30.4 all-gather.5
  42.3 23.3 all-gather.7
  248.9 23.7 all-gather.9
